TPU v7x, 32 devices: a whole 2x2x4 slice. The times are simulated.
32 devices in a mesh: expert: 16 (over z, x, core), tensor: 2 (over y).
Axes of the slice: x: 2, y: 2, z: 4, core: 2. Of those that a mesh axis runs over, the one named last changes fastest.
Arguments:
- tokens: bfloat16 [256, 7168], P('expert'), may hold values from -6 to 6
- routes: int32 [256, 8], P('expert'), may hold values from 0 to 15, all different within a row; in each aligned block of 16 rows (0 to 15, 16 to 31, ...) at most 8 rows name the same one
- route_logits: float32 [256, 8], P('expert'), may hold values from -8 to 8
- gate_weight: bfloat16 [16, 7168, 1024], P('expert', 'tensor'), may hold values from -0.0625 to 0.0625
- up_weight: bfloat16 [16, 7168, 1024], P('expert', 'tensor'), may hold values from -0.0625 to 0.0625
- down_weight: bfloat16 [16, 7168, 1024], P('expert', 'tensor'), may hold values from -0.1875 to 0.1875
Outputs:
- mixed: bfloat16 [256, 7168], P('expert', 'tensor')
Inputs may be any that keep to these rules, and one draw needn't show every extreme that they name: `routes`: each row names 8 different experts. In each aligned block of 16 rows (the rows of one index of expert) no expert is named by more than 8 rows, a bound that some block reaches.
All inputs are finite; a program needn't handle non-finite values.
Results may differ from a plain program's by a relative error of at most 0.0066.
Values may be sent and summed in bfloat16 or wider, within the bound.
A program may use at most 64 MiB of HBM per device.

v0:
```python
import functools

import jax
import jax.numpy as jnp
from jax import lax
from jax.experimental import pallas as pl
from jax.experimental.pallas import tpu as pltpu
from jax.sharding import PartitionSpec as P

routed_scale = 2.5
MESH = pl.DeviceIdType.MESH
BF = jnp.bfloat16
F32 = jnp.float32


def kernel(
    dims,
    tokens_ref,
    routes_ref,
    logits_ref,
    gate_hbm,
    up_hbm,
    down_hbm,
    out_ref,
    G,
    gw,
    uw,
    dw,
    X,
    ysend,
    yrecv,
    hid,
    dense,
    crecv,
    s1,
    xrecv,
    s2,
    zrecv,
    wsem,
    tsem,
    grecv,
    gz,
    gx,
    gc,
    ys,
    yr,
    hs,
    hr,
    cs,
    cr,
    xs,
    xr,
    zs,
    zr,
):
    E, T, A, B, tok, cap, top, Dl, F, lanes, nd, dc, fc, nj, pieces = dims
    R, NT, FT = E * cap, E * tok, F // T
    e = lax.axis_index("expert")
    t = lax.axis_index("tensor")
    c = lax.rem(e, 2)
    b = lax.rem(e // 2, B)
    a = e // (2 * B)

    def around(v, i, n):
        return lax.rem(v + i, n)

    def slot_of(ai, bi, ci):
        return (ai * B + bi) * 2 + ci

    def dev(ai, bi, ci):
        return (slot_of(ai, bi, ci), t)

    half = Dl // 256 * 128
    spans = ((0, half), (half, Dl - half))
    barrier = pltpu.get_barrier_semaphore()
    partners = [dev(around(a, i, A), b, c) for i in range(1, A)]
    partners += [dev(a, around(b, k, B), c) for k in range(1, B)]
    partners += [dev(a, b, 1 - c)]
    partners += [(e, around(t, p, T)) for p in range(1, T)]
    for partner in partners:
        pl.semaphore_signal(barrier, inc=1, device_id=partner, device_id_type=MESH)

    token_copies = []
    for h, (first, width) in enumerate(spans):
        copy = pltpu.make_async_copy(
            tokens_ref.at[:, pl.ds(pl.multiple_of(t * Dl + first, 128), width)],
            G.at[pl.ds(pl.multiple_of(e * tok, tok), tok), pl.ds(first, width)],
            tsem.at[h],
        )
        copy.start()
        token_copies.append(copy)

    step_in, step_out = Dl // pieces, Dl // pieces
    weight_copies = []
    for which, (src, dst) in enumerate(((gate_hbm, gw), (up_hbm, uw), (down_hbm, dw))):
        for p in range(pieces):
            rows = pl.ds(p * step_in, step_in)
            copy = pltpu.make_async_copy(src.at[0, rows], dst.at[rows], wsem.at[which, p])
            copy.start()
            weight_copies.append(copy)

    scores = jax.nn.sigmoid(logits_ref[...])
    weights = routed_scale * scores / jnp.sum(scores, axis=0, keepdims=True)
    routes = routes_ref[...]
    lane = lax.broadcasted_iota(jnp.int32, (lanes, tok), 0)
    table = jnp.zeros((lanes, tok), F32)
    for k in range(top):
        table += jnp.where(lane == routes[k : k + 1], weights[k : k + 1], 0.0)
    high = table.astype(BF)
    low = (table - high.astype(F32)).astype(BF)
    nt = (((1,), (1,)), ((), ()))
    unit = lax.broadcasted_iota(jnp.int32, (tok, tok), 0) == lax.broadcasted_iota(jnp.int32, (tok, tok), 1)
    unit = jnp.where(unit, 1.0, 0.0).astype(BF)
    high = lax.dot_general(unit, high, nt, preferred_element_type=F32).astype(BF)
    low = lax.dot_general(unit, low, nt, preferred_element_type=F32).astype(BF)

    def block(slot):
        return pl.ds(pl.multiple_of(slot * tok, tok), tok)

    G[block(e), pl.ds(Dl, lanes)] = high
    G[block(e), pl.ds(Dl + lanes, lanes)] = low
    pl.semaphore_wait(barrier, len(partners))
    for copy in token_copies:
        copy.wait()

    parts = ((0, half), (half, Dl - half + 2 * lanes))

    def gcopy(slot, h, target, sem):
        cols = pl.ds(*parts[h])
        return pltpu.make_async_remote_copy(
            src_ref=G.at[block(slot), cols],
            dst_ref=G.at[block(slot), cols],
            send_sem=sem,
            recv_sem=grecv.at[slot, h],
            device_id=target,
            device_id_type=MESH,
        )

    sibling = dev(a, b, 1 - c)

    def spread(h, s, d, upward, downward):
        slot = slot_of(a + d, b, c)
        if d:
            gcopy(slot, h, sibling, gc.at[s, 0, h]).wait_recv()
        if upward:

            @pl.when(a < A - 1)
            def _():
                gcopy(slot, h, dev(a + 1, b, c), gz.at[0, s, h]).start()

        if downward:

            @pl.when(a > 0)
            def _():
                gcopy(slot, h, dev(a - 1, b, c), gz.at[1, s, h]).start()

        for k in range(1, B):
            gcopy(slot, h, dev(a, around(b, k, B), c), gx.at[a + d, k, h]).start()
        gcopy(slot, h, sibling, gc.at[a + d, 0, h]).start()

    for s in range(A):
        for h in range(2):
            if s == 0:
                spread(h, 0, 0, True, True)
            else:

                @pl.when(a - s >= 0)
                def _():
                    spread(h, s, -s, True, False)

                @pl.when(a + s < A)
                def _():
                    spread(h, s, s, False, True)

    for s in range(A):
        for h in range(2):
            for sign in (-1, 1) if s else (1,):

                @pl.when((a + sign * s >= 0) & (a + sign * s < A))
                def _():
                    at = a + sign * s
                    for k in range(1, B):
                        copy = gcopy(slot_of(at, around(b, k, B), c), h, sibling, gc.at[at, k, h])
                        copy.wait_recv()
                        copy.start()

    for i in range(A):
        for k in range(B):
            for h in range(2):
                gcopy(slot_of(i, around(b, k, B), 1 - c), h, sibling, gc.at[i, k, h]).wait_recv()

    high = G[:, pl.ds(Dl, lanes)]
    low = G[:, pl.ds(Dl + lanes, lanes)]
    pick = (lax.broadcasted_iota(jnp.int32, (8, lanes), 1) == e).astype(F32).astype(BF)
    wrow = lax.dot_general(pick, high, nt, preferred_element_type=F32) + lax.dot_general(
        pick, low, nt, preferred_element_type=F32
    )
    sub = lax.broadcasted_iota(jnp.int32, (NT, NT), 0)
    lan = lax.broadcasted_iota(jnp.int32, (NT, NT), 1)
    same = (sub // tok) == (lan // tok)
    before_row = jnp.where(same & (sub < lan), 1.0, 0.0).astype(BF)
    before_col = jnp.where(same & (lan < sub), 1.0, 0.0).astype(BF)
    row_on = jnp.where(wrow > 0, 1.0, 0.0)
    row_pos = jnp.dot(row_on.astype(BF), before_row, preferred_element_type=F32)
    row_blk = (lax.broadcasted_iota(jnp.int32, (8, NT), 1) // tok * cap).astype(F32)
    row_at = jnp.where(wrow > 0, row_blk + row_pos, -1.0)[:1]
    slot_row = lax.broadcasted_iota(jnp.int32, (R, NT), 0).astype(F32)
    chosen = jnp.where(slot_row == row_at, 1.0, 0.0)
    wslot = jnp.sum(chosen * wrow[:1], axis=1, keepdims=True)
    S = chosen.astype(BF)

    mine = lax.broadcasted_iota(jnp.int32, (NT, lanes), 1) == e
    full = high.astype(F32) + low.astype(F32)
    all_on = jnp.where(full > 0, 1.0, 0.0)
    col_pos = jnp.dot(before_col, all_on.astype(BF), preferred_element_type=F32)
    col_blk = (lax.broadcasted_iota(jnp.int32, (NT, lanes), 0) // tok * cap).astype(F32)
    col_at = jnp.where(full > 0, col_blk + col_pos, -1.0)
    col_at = jnp.sum(jnp.where(mine, col_at, 0.0), axis=1, keepdims=True)
    slot_col = lax.broadcasted_iota(jnp.int32, (NT, R), 1).astype(F32)
    ST = jnp.where(slot_col == col_at, 1.0, 0.0).astype(BF)

    for copy in weight_copies:
        copy.wait()

    @pl.loop(0, nd)
    def _(j):
        cols = pl.ds(pl.multiple_of(j * dc, 128), dc)
        X[:, cols] = jnp.dot(S, G[:, cols], preferred_element_type=F32).astype(BF)

    def ycopy(p, j):
        return pltpu.make_async_remote_copy(
            src_ref=ysend.at[p - 1, j],
            dst_ref=yrecv.at[p - 1, j],
            send_sem=ys.at[p - 1, j],
            recv_sem=yr.at[p - 1, j],
            device_id=(e, around(t, p, T)),
            device_id_type=MESH,
        )

    def hcols(rank, j):
        return pl.ds(pl.multiple_of(rank * FT + j * fc, 128), fc)

    def hcopy(p, j, rank):
        return pltpu.make_async_remote_copy(
            src_ref=hid.at[:, hcols(rank, j)],
            dst_ref=hid.at[:, hcols(rank, j)],
            send_sem=hs.at[p - 1, j],
            recv_sem=hr.at[p - 1, j],
            device_id=(e, around(t, p, T)),
            device_id_type=MESH,
        )

    for p in range(1, T):

        @pl.loop(0, nj)
        def _(j):
            cols = hcols(around(t, p, T), j)
            g = jnp.dot(X[...], gw[:, cols], preferred_element_type=F32)
            u = jnp.dot(X[...], uw[:, cols], preferred_element_type=F32)
            ysend[p - 1, j, 0] = g.astype(BF)
            ysend[p - 1, j, 1] = u.astype(BF)
            ycopy(p, j).start()

    @pl.loop(0, nj)
    def _(j):
        cols = hcols(t, j)
        g = jnp.dot(X[...], gw[:, cols], preferred_element_type=F32)
        u = jnp.dot(X[...], uw[:, cols], preferred_element_type=F32)
        for p in range(1, T):
            ycopy(p, j).wait_recv()
            g += yrecv[p - 1, j, 0].astype(F32)
            u += yrecv[p - 1, j, 1].astype(F32)
        hid[:, cols] = (g / (1.0 + jnp.exp(-g)) * u).astype(BF)
        for p in range(1, T):
            hcopy(p, j, t).start()

    for p in range(1, T):
        for j in range(nj):
            hcopy(p, j, around(t, T - p, T)).wait_recv()

    def ccopy(j):
        return pltpu.make_async_remote_copy(
            src_ref=dense.at[j, 1 - c],
            dst_ref=crecv.at[j],
            send_sem=cs.at[j],
            recv_sem=cr.at[j],
            device_id=dev(a, b, 1 - c),
            device_id_type=MESH,
        )

    def xcopy(j, k):
        return pltpu.make_async_remote_copy(
            src_ref=s1.at[j, around(b, k, B)],
            dst_ref=xrecv.at[j, k - 1],
            send_sem=xs.at[j, k - 1],
            recv_sem=xr.at[j, k - 1],
            device_id=dev(a, around(b, k, B), c),
            device_id_type=MESH,
        )

    def zcopy(j, i):
        return pltpu.make_async_remote_copy(
            src_ref=s2.at[j, around(a, i, A)],
            dst_ref=zrecv.at[j, i - 1],
            send_sem=zs.at[j, i - 1],
            recv_sem=zr.at[j, i - 1],
            device_id=dev(around(a, i, A), b, c),
            device_id_type=MESH,
        )

    @pl.loop(0, nd + 4)
    def _(step):
        @pl.when(step < nd)
        def _():
            j = step
            rows = pl.ds(pl.multiple_of(j * dc, 128), dc)
            y = lax.dot_general(hid[...], dw[rows, :], nt, preferred_element_type=F32)
            y = (y * wslot).astype(BF)
            back = jnp.dot(ST, y, preferred_element_type=F32).astype(BF)
            for slot in range(E):
                at = (slot // 2 % B) * A + slot // (2 * B)
                dense[j, slot % 2, at * tok : (at + 1) * tok, :] = back[slot * tok : (slot + 1) * tok]
            ccopy(j).start()

        @pl.when((step >= 1) & (step < nd + 1))
        def _():
            j = step - 1
            ccopy(j).wait_recv()
            for k in range(B):
                at = pl.ds(k * A * tok, A * tok)
                s1[j, k] = (dense[j, c, at].astype(F32) + crecv[j, at].astype(F32)).astype(BF)
            for k in range(1, B):
                xcopy(j, k).start()

        @pl.when(step >= 4)
        def _():
            j = step - 4
            for k in range(1, B):
                xcopy(j, k).wait_recv()
            for i in range(A):
                at = pl.ds(i * tok, tok)
                total = s1[j, b, at].astype(F32)
                for k in range(1, B):
                    total += xrecv[j, k - 1, at].astype(F32)
                s2[j, i] = total.astype(BF)
            for i in range(1, A):
                zcopy(j, i).start()

    @pl.loop(0, nd)
    def _(j):
        total = s2[j, a].astype(F32)
        for i in range(1, A):
            zcopy(j, i).wait_recv()
            total += zrecv[j, i - 1].astype(F32)
        out_ref[:, pl.ds(pl.multiple_of(j * dc, 128), dc)] = total.astype(BF)

    for h in range(2):
        for s in range(A):

            @pl.when((a - s >= 0) & (a < A - 1))
            def _():
                gcopy(e, h, sibling, gz.at[0, s, h]).wait_send()

            @pl.when((a + s < A) & (a > 0))
            def _():
                gcopy(e, h, sibling, gz.at[1, s, h]).wait_send()

            for k in range(B):
                gcopy(e, h, sibling, gc.at[s, k, h]).wait_send()
                if k:
                    gcopy(e, h, sibling, gx.at[s, k, h]).wait_send()

    for p in range(1, T):
        for j in range(nj):
            ycopy(p, j).wait_send()
            hcopy(p, j, t).wait_send()

    @pl.loop(0, nd)
    def _(j):
        ccopy(j).wait_send()
        for k in range(1, B):
            xcopy(j, k).wait_send()
        for i in range(1, A):
            zcopy(j, i).wait_send()


def shards(tokens, routes, route_logits, gate_weight, up_weight, down_weight):
    E = lax.axis_size("expert")
    T = lax.axis_size("tensor")
    tok, D = tokens.shape
    top = routes.shape[1]
    _, Dl, F = gate_weight.shape
    cap = tok // 2
    A = 4
    B = E // (2 * A)
    assert E == A * B * 2 and D == Dl * T
    lanes = -(-E // 128) * 128
    nd = 7 if Dl % (7 * 128) == 0 else 1
    dc = Dl // nd
    FT = F // T
    fc = 128 if FT % 128 == 0 else FT
    nj = FT // fc
    pieces = 4
    R, NT = E * cap, E * tok
    dims = (E, T, A, B, tok, cap, top, Dl, F, lanes, nd, dc, fc, nj, pieces)
    vmem = pl.BlockSpec(memory_space=pltpu.VMEM)
    hbm = pl.BlockSpec(memory_space=pl.ANY)
    dma = pltpu.SemaphoreType.DMA
    return pl.pallas_call(
        functools.partial(kernel, dims),
        out_shape=jax.ShapeDtypeStruct((tok, Dl), BF),
        in_specs=[hbm, vmem, vmem, hbm, hbm, hbm],
        out_specs=vmem,
        scratch_shapes=[
            pltpu.VMEM((NT, Dl + 2 * lanes), BF),
            pltpu.VMEM((Dl, F), BF),
            pltpu.VMEM((Dl, F), BF),
            pltpu.VMEM((Dl, F), BF),
            pltpu.VMEM((R, Dl), BF),
            pltpu.VMEM((T - 1, nj, 2, R, fc), BF),
            pltpu.VMEM((T - 1, nj, 2, R, fc), BF),
            pltpu.VMEM((R, F), BF),
            pltpu.VMEM((nd, 2, A * B * tok, dc), BF),
            pltpu.VMEM((nd, A * B * tok, dc), BF),
            pltpu.VMEM((nd, B, A * tok, dc), BF),
            pltpu.VMEM((nd, B - 1, A * tok, dc), BF),
            pltpu.VMEM((nd, A, tok, dc), BF),
            pltpu.VMEM((nd, A - 1, tok, dc), BF),
            dma((3, pieces)),
            dma((2,)),
            dma((E, 2)),
            dma((2, A, 2)),
            dma((A, B, 2)),
            dma((A, B, 2)),
            dma((T - 1, nj)),
            dma((T - 1, nj)),
            dma((T - 1, nj)),
            dma((T - 1, nj)),
            dma((nd,)),
            dma((nd,)),
            dma((nd, B - 1)),
            dma((nd, B - 1)),
            dma((nd, A - 1)),
            dma((nd, A - 1)),
        ],
        compiler_params=pltpu.CompilerParams(
            collective_id=0, has_side_effects=True, vmem_limit_bytes=60 * 1024 * 1024
        ),
    )(tokens, routes.T, route_logits.T, gate_weight, up_weight, down_weight)


def solution(mesh):
    return jax.shard_map(
        shards,
        mesh=mesh,
        in_specs=(
            P("expert", None),
            P("expert", None),
            P("expert", None),
            P("expert", "tensor", None),
            P("expert", "tensor", None),
            P("expert", "tensor", None),
        ),
        out_specs=P("expert", "tensor"),
        check_vma=False,
    )
```

profile of v0, /device:TPU:0, one launch (start us, length us, event | category | flops | bytes accessed | tf_op | source)
XLA Modules:
  0.0 56.8 jit_solution(2984061606919007448)
XLA Ops:
  0.0 55.3 %shard_map.64 = bf16[16,3584]{1,0:T(8,128)(2,1)} custom-call(bf16[16,7168]{1,0:T(8,128)(2,1)} %tokens_ref.1, s32[8,16]{1,0:T(8,128)} %bitcast.2, f32[8,16]{1,0:T(8,128)} %bitcast.3, bf16[1,3584,1024]{2,1,0:T(8,128)(2,1)} %gate_hbm.1, bf16[1,3584,1024]{2,1,0:T(8,128)(2,1)} %up_hbm.1, bf16[1,3584,1024]{2,1,0:T(8,128)(2,1)} %down_hbm.1), custom_call_target="tpu_custom_call" | custom-call | tf_op jit(solution)/shard_map/pallas_call | solution.py:409
  55.3 1.6 %copy.8 = bf16[16,3584]{1,0:T(8,128)(2,1)} copy(bf16[16,3584]{1,0:T(8,128)(2,1)} %shard_map.64) | data formatting | bytes 229376
where the time goes:
time: 57 us; the launch traced here: 56.8 us
  Pallas kernels  55.3 us (97%)
  local copies, waits for them, and re-layouts  1.55 us (3%)
    pallas_call x1, Pallas kernels, shards(): pl.pallas_call(functools.partial(kernel, dims), out_shape=jax.ShapeDtypeS...  55.3 us
    unnamed x1, local copies, waits for them, and re-layouts  1.55 us

commit v1 on v0

--- a/solution.py
+++ b/solution.py
@@ -90,15 +90,6 @@
         copy.start()
         token_copies.append(copy)
 
-    step_in, step_out = Dl // pieces, Dl // pieces
-    weight_copies = []
-    for which, (src, dst) in enumerate(((gate_hbm, gw), (up_hbm, uw), (down_hbm, dw))):
-        for p in range(pieces):
-            rows = pl.ds(p * step_in, step_in)
-            copy = pltpu.make_async_copy(src.at[0, rows], dst.at[rows], wsem.at[which, p])
-            copy.start()
-            weight_copies.append(copy)
-
     scores = jax.nn.sigmoid(logits_ref[...])
     weights = routed_scale * scores / jnp.sum(scores, axis=0, keepdims=True)
     routes = routes_ref[...]
@@ -122,6 +113,15 @@
     pl.semaphore_wait(barrier, len(partners))
     for copy in token_copies:
         copy.wait()
+
+    step_in, step_out = Dl // pieces, Dl // pieces
+    weight_copies = []
+    for which, (src, dst) in enumerate(((gate_hbm, gw), (up_hbm, uw), (down_hbm, dw))):
+        for p in range(pieces):
+            rows = pl.ds(p * step_in, step_in)
+            copy = pltpu.make_async_copy(src.at[0, rows], dst.at[rows], wsem.at[which, p])
+            copy.start()
+            weight_copies.append(copy)
 
     parts = ((0, half), (half, Dl - half + 2 * lanes))
 

time: 57 us -> 54.8 us (0.961)
  Pallas kernels: 55.3 us -> 53.1 us
    pallas_call x1, Pallas kernels: 55.3 us -> 53.1 us  [shards(): pl.pallas_call(functools.partial(kernel, dims), out_shape=jax.ShapeDtypeS...]
where the time goes in v1:
time: 54.8 us; the launch traced here: 54.7 us
  Pallas kernels  53.1 us (97%)
  local copies, waits for them, and re-layouts  1.55 us (3%)
    pallas_call x1, Pallas kernels, shards(): pl.pallas_call(functools.partial(kernel, dims), out_shape=jax.ShapeDtypeS...  53.1 us
    unnamed x1, local copies, waits for them, and re-layouts  1.55 us

profile of v1, /device:TPU:0, one launch (start us, length us, event | category | flops | bytes accessed | tf_op | source)
XLA Modules:
  0.0 54.7 jit_solution(13998611350666677222)
XLA Ops:
  0.0 53.1 %shard_map.64 = bf16[16,3584]{1,0:T(8,128)(2,1)} custom-call(bf16[16,7168]{1,0:T(8,128)(2,1)} %tokens_ref.1, s32[8,16]{1,0:T(8,128)} %bitcast.2, f32[8,16]{1,0:T(8,128)} %bitcast.3, bf16[1,3584,1024]{2,1,0:T(8,128)(2,1)} %gate_hbm.1, bf16[1,3584,1024]{2,1,0:T(8,128)(2,1)} %up_hbm.1, bf16[1,3584,1024]{2,1,0:T(8,128)(2,1)} %down_hbm.1), custom_call_target="tpu_custom_call" | custom-call | tf_op jit(solution)/shard_map/pallas_call | solution.py:409
  53.1 1.6 %copy.8 = bf16[16,3584]{1,0:T(8,128)(2,1)} copy(bf16[16,3584]{1,0:T(8,128)(2,1)} %shard_map.64) | data formatting | bytes 229376

commit v2 on v1

v2 whole, which is shorter than its diff:
```python
import functools

import jax
import jax.numpy as jnp
from jax import lax
from jax.experimental import pallas as pl
from jax.experimental.pallas import tpu as pltpu
from jax.sharding import PartitionSpec as P

routed_scale = 2.5
MESH = pl.DeviceIdType.MESH
BF = jnp.bfloat16
F32 = jnp.float32
NT_DIMS = (((1,), (1,)), ((), ()))
CORE_LAG, X_LAG, Z_LAG = 2, 6, 9
HELD = 0


def kernel(
    dims,
    tokens_ref,
    routes_hbm,
    logits_hbm,
    gate_hbm,
    up_hbm,
    down_hbm,
    out_ref,
    routes_ref,
    logits_ref,
    G,
    gw,
    uw,
    dw,
    X,
    spread_back,
    wslot,
    ysend,
    yrecv,
    acc,
    hid,
    dense,
    crecv,
    s1,
    xrecv,
    s2,
    z1recv,
    s3,
    z2recv,
    rsem,
    wsem,
    tsem,
    gs,
    gzr,
    gxr,
    gcr,
    ys,
    yr,
    hs,
    hr,
    cs,
    cr,
    xs,
    xr,
    z1s,
    z1r,
    z2s,
    z2r,
):
    E, T, A, B, tok, cap, top, Dl, F, lanes, hc, nd, dc, fc, nj, pieces = dims
    slots = 2 * B * 2
    NG, RG, FT = slots * tok, slots * cap, F // T
    hw = Dl // hc
    e = lax.axis_index("expert")
    t = lax.axis_index("tensor")
    c = lax.rem(e, 2)
    b = lax.rem(e // 2, B)
    a = e // (2 * B)
    r = lax.rem(a, 2)
    half = a // 2
    near = a + 1 - 2 * r
    far = a + 2 - 4 * half
    places = (a, near, far, far + 1 - 2 * r)

    def around(v, i, n):
        return lax.rem(v + i, n)

    def slot_of(ai, bi, ci):
        return (ai * B + bi) * 2 + ci

    def dev(ai, bi, ci):
        return (slot_of(ai, bi, ci), t)

    sibling = dev(a, b, 1 - c)
    z1, z2 = dev(near, b, c), dev(far, b, c)

    barrier = pltpu.get_barrier_semaphore()
    partners = [z1, z2, sibling]
    partners += [dev(a, around(b, k, B), c) for k in range(1, B)]
    partners += [(e, around(t, p, T)) for p in range(1, T)]
    for partner in partners:
        pl.semaphore_signal(barrier, inc=1, device_id=partner, device_id_type=MESH)

    def block(slot):
        return pl.ds(pl.multiple_of(slot * tok, tok), tok)

    route_copies = []
    for which, (src, dst) in enumerate(((routes_hbm, routes_ref), (logits_hbm, logits_ref))):
        copy = pltpu.make_async_copy(src, dst, rsem.at[which])
        copy.start()
        route_copies.append(copy)
    token_copies = []
    for h in range(hc):
        copy = pltpu.make_async_copy(
            tokens_ref.at[:, pl.ds(pl.multiple_of(t * Dl + h * hw, 128), hw)],
            G.at[block(e), pl.ds(lanes + h * hw, hw)],
            tsem.at[h],
        )
        copy.start()
        token_copies.append(copy)

    low_at = lanes // 2
    for copy in route_copies:
        copy.wait()
    scores = jax.nn.sigmoid(logits_ref[...])
    weights = routed_scale * scores / jnp.sum(scores, axis=0, keepdims=True)
    routes = routes_ref[...]
    lane = lax.broadcasted_iota(jnp.int32, (low_at, tok), 0)
    table = jnp.zeros((low_at, tok), F32)
    for k in range(top):
        table += jnp.where(lane == routes[k : k + 1], weights[k : k + 1], 0.0)
    high = table.astype(BF)
    low = (table - high.astype(F32)).astype(BF)
    unit = lax.broadcasted_iota(jnp.int32, (tok, tok), 0) == lax.broadcasted_iota(jnp.int32, (tok, tok), 1)
    unit = jnp.where(unit, 1.0, 0.0).astype(BF)
    both = jnp.concatenate([high, low], axis=0)
    G[block(e), pl.ds(0, lanes)] = lax.dot_general(unit, both, NT_DIMS, preferred_element_type=F32).astype(BF)

    sub = lax.broadcasted_iota(jnp.int32, (NG, NG), 0)
    lan = lax.broadcasted_iota(jnp.int32, (NG, NG), 1)
    same = (sub // tok) == (lan // tok)
    before_row = jnp.where(same & (sub < lan), 1.0, 0.0).astype(BF)
    before_col = jnp.where(same & (lan < sub), 1.0, 0.0).astype(BF)

    pl.semaphore_wait(barrier, len(partners))

    def part(h):
        if isinstance(h, int) and h == 0:
            return pl.ds(0, lanes + hw)
        return pl.ds(pl.multiple_of(lanes + h * hw, 128), hw)

    def gcopy(slot, h, target, sem):
        return pltpu.make_async_remote_copy(
            src_ref=G.at[block(slot), part(h)],
            dst_ref=G.at[block(slot), part(h)],
            send_sem=gs,
            recv_sem=sem,
            device_id=target,
            device_id_type=MESH,
        )

    def gwait(h, sem, count=1):
        span = G.at[pl.ds(0, count * tok), part(h)]
        pltpu.make_async_copy(span, span, sem).wait()

    def across(i, h):
        slot = slot_of(places[i], b, c)
        for k in range(1, B):
            gcopy(slot, h, dev(a, around(b, k, B), c), gxr.at[i, k - 1, h]).start()
        gcopy(slot, h, sibling, gcr.at[i // 2, h]).start()

    def relay(i, h):
        for k in range(1, B):
            gwait(h, gxr.at[i, k - 1, h])
            gcopy(slot_of(places[i], around(b, B - k, B), c), h, sibling, gcr.at[i // 2, h]).start()

    for h in range(hc):
        token_copies[h].wait()
        gcopy(e, h, z1, gzr.at[0, h]).start()
        across(0, h)

    step_in = Dl // pieces
    for which, (src, dst) in enumerate(((gate_hbm, gw), (up_hbm, uw), (down_hbm, dw))):
        for p in range(pieces):
            rows = pl.ds(p * step_in, step_in)
            pltpu.make_async_copy(src.at[0, rows], dst.at[rows], wsem.at[which]).start()

    def weight_ready(which, src, dst):
        pltpu.make_async_copy(src.at[0], dst, wsem.at[which]).wait()

    for h in range(hc):
        gwait(h, gzr.at[0, h])
        across(1, h)
        gcopy(e, h, z2, gzr.at[1, h]).start()
        relay(0, h)

    for h in range(hc):
        gwait(h, gzr.at[1, h])
        gcopy(slot_of(far, b, c), h, z1, gzr.at[2, h]).start()
        across(2, h)
        relay(1, h)

    def relay_far(h):
        gwait(h, gzr.at[2, h])
        across(3, h)
        relay(2, h)

    def relay_last(h):
        relay(3, h)

    def group_rows(g):
        return pl.ds(pl.multiple_of((half if g == 0 else 1 - half) * NG, NG), NG)

    def choose(g):
        meta = G[group_rows(g), pl.ds(0, lanes)]
        at = lax.broadcasted_iota(jnp.int32, (8, lanes), 1)
        pick = jnp.where((at == e) | (at == e + low_at), 1.0, 0.0).astype(BF)
        wrow = lax.dot_general(pick, meta, NT_DIMS, preferred_element_type=F32)
        row_on = jnp.where(wrow > 0, 1.0, 0.0)
        row_pos = jnp.dot(row_on.astype(BF), before_row, preferred_element_type=F32)
        row_blk = (lax.broadcasted_iota(jnp.int32, (8, NG), 1) // tok * cap).astype(F32)
        row_at = jnp.where(wrow > 0, row_blk + row_pos, -1.0)[:1]
        slot_row = lax.broadcasted_iota(jnp.int32, (RG, NG), 0).astype(F32)
        S = jnp.where(slot_row == row_at, 1.0, 0.0).astype(BF)

        full = meta.astype(F32)
        at = lax.broadcasted_iota(jnp.int32, (NG, lanes), 1)
        all_on = jnp.where(full > 0, 1.0, 0.0)
        col_pos = jnp.dot(before_col, all_on.astype(BF), preferred_element_type=F32)
        col_blk = (lax.broadcasted_iota(jnp.int32, (NG, lanes), 0) // tok * cap).astype(F32)
        col_at = jnp.where(full > 0, col_blk + col_pos, -1.0)
        col_at = jnp.sum(jnp.where(at == e, col_at, 0.0), axis=1, keepdims=True)
        slot_col = lax.broadcasted_iota(jnp.int32, (NG, RG), 1).astype(F32)
        spread_back[g] = jnp.where(slot_col == col_at, 1.0, 0.0).astype(BF)
        mine = (at == e) | (at == e + low_at)
        wcol = jnp.sum(jnp.where(mine, full, 0.0), axis=1, keepdims=True)
        wslot[g] = jnp.sum(jnp.where(slot_col == col_at, wcol, 0.0), axis=0, keepdims=True)
        return S

    chosen = [None, None]

    def collect(g, h):
        gwait(h, gcr.at[g, h], 2 * B)
        if h == 0:
            chosen[g] = choose(g)
        rows = G[group_rows(g), pl.ds(lanes + h * hw, hw)]
        X[g, :, pl.ds(h * hw, hw)] = jnp.dot(chosen[g], rows, preferred_element_type=F32).astype(BF)

    def ycopy(g, p, j):
        return pltpu.make_async_remote_copy(
            src_ref=ysend.at[g, p - 1, j],
            dst_ref=yrecv.at[g, p - 1, j],
            send_sem=ys,
            recv_sem=yr.at[g, p - 1, j],
            device_id=(e, around(t, p, T)),
            device_id_type=MESH,
        )

    def hcols(rank, j):
        return pl.ds(pl.multiple_of(rank * FT + j * fc, 128), fc)

    def hcopy(g, p, j, rank):
        return pltpu.make_async_remote_copy(
            src_ref=hid.at[g, :, hcols(rank, j)],
            dst_ref=hid.at[g, :, hcols(rank, j)],
            send_sem=hs,
            recv_sem=hr.at[g],
            device_id=(e, around(t, p, T)),
            device_id_type=MESH,
        )

    def gate_up_theirs(g, j):
        for p in range(1, T):
            cols = hcols(around(t, p, T), j)
            ysend[g, p - 1, j, 0] = jnp.dot(X[g], gw[:, cols], preferred_element_type=F32).astype(BF)
            ysend[g, p - 1, j, 1] = jnp.dot(X[g], uw[:, cols], preferred_element_type=F32).astype(BF)
            ycopy(g, p, j).start()

    def gate_up_own(g, j):
        cols = hcols(t, j)
        acc[g, j, 0] = jnp.dot(X[g], gw[:, cols], preferred_element_type=F32)
        acc[g, j, 1] = jnp.dot(X[g], uw[:, cols], preferred_element_type=F32)

    def hidden(g, j):
        gv, uv = acc[g, j, 0], acc[g, j, 1]
        for p in range(1, T):
            ycopy(g, p, j).wait_recv()
            gv += yrecv[g, p - 1, j, 0].astype(F32)
            uv += yrecv[g, p - 1, j, 1].astype(F32)
        hid[g, :, hcols(t, j)] = (gv / (1.0 + jnp.exp(-gv)) * uv).astype(BF)
        for p in range(1, T):
            hcopy(g, p, j, t).start()

    def hidden_ready(g):
        span = hid.at[g, :, pl.ds(0, F - FT)]
        pltpu.make_async_copy(span, span, hr.at[g]).wait()

    def spread_over(work, side):
        for i, item in enumerate(work):
            item()
            for other in side[i * len(side) // len(work) : (i + 1) * len(side) // len(work)]:
                other()

    def each(fn, n, *lead):
        return [functools.partial(fn, *lead, i) for i in range(n)]

    for h in range(hc):
        collect(0, h)
    weight_ready(0, gate_hbm, gw)
    weight_ready(1, up_hbm, uw)
    spread_over(each(gate_up_theirs, nj, 0), each(relay_far, hc))
    for j in range(nj):
        gate_up_own(0, j)
    spread_over(each(relay_last, hc), each(hidden, nj, 0))
    for h in range(hc):
        collect(1, h)
    for j in range(nj):
        gate_up_theirs(1, j)

    def ccopy(j):
        return pltpu.make_async_remote_copy(
            src_ref=dense.at[j, 1 - c],
            dst_ref=crecv.at[j],
            send_sem=cs,
            recv_sem=cr.at[j],
            device_id=sibling,
            device_id_type=MESH,
        )

    def xcopy(j, k):
        return pltpu.make_async_remote_copy(
            src_ref=s1.at[j, around(b, k, B)],
            dst_ref=xrecv.at[j, k - 1],
            send_sem=xs,
            recv_sem=xr.at[j],
            device_id=dev(a, around(b, k, B), c),
            device_id_type=MESH,
        )

    def z1copy(j):
        return pltpu.make_async_remote_copy(
            src_ref=s2.at[j, 1 - r],
            dst_ref=z1recv.at[j],
            send_sem=z1s,
            recv_sem=z1r.at[j],
            device_id=z1,
            device_id_type=MESH,
        )

    def z2copy(j):
        return pltpu.make_async_remote_copy(
            src_ref=s3.at[j],
            dst_ref=z2recv.at[j],
            send_sem=z2s,
            recv_sem=z2r.at[j],
            device_id=z2,
            device_id_type=MESH,
        )

    total_steps = 2 * nd
    nd_before = max(nd - HELD, 1)

    def down(g, step, early=True):
        j = step - nd_before if g else step if early else step - nd
        rows = pl.ds(pl.multiple_of(j * dc, 128), dc)
        y = lax.dot_general(dw[rows, :], hid[g], NT_DIMS, preferred_element_type=F32)
        y = (y * wslot[g]).astype(BF)
        y = lax.dot_general(spread_back[g], y, NT_DIMS, preferred_element_type=F32).astype(BF)
        for slot in range(slots):
            at = (slot // 2 % B) * 2 + slot // (2 * B)
            dense[step, slot % 2, at * tok : (at + 1) * tok, :] = y[slot * tok : (slot + 1) * tok]
        ccopy(step).start()

    def reduce_steps(step):
        @pl.when((step >= CORE_LAG) & (step < total_steps + CORE_LAG))
        def _():
            j = step - CORE_LAG
            ccopy(j).wait_recv()
            for k in range(B):
                at = pl.ds(k * 2 * tok, 2 * tok)
                s1[j, k] = (dense[j, c, at].astype(F32) + crecv[j, at].astype(F32)).astype(BF)
            for k in range(1, B):
                xcopy(j, k).start()

        @pl.when((step >= X_LAG) & (step < total_steps + X_LAG))
        def _():
            j = step - X_LAG
            pltpu.make_async_copy(xrecv.at[j], xrecv.at[j], xr.at[j]).wait()
            for i in range(2):
                at = pl.ds(i * tok, tok)
                total = s1[j, b, at].astype(F32)
                for k in range(1, B):
                    total += xrecv[j, k - 1, at].astype(F32)
                s2[j, i] = total.astype(BF)
            z1copy(j).start()

        @pl.when((step >= Z_LAG + nd_before) & (step < nd_before + nd + Z_LAG))
        def _():
            j = step - Z_LAG
            z1copy(j).wait_recv()
            s3[j - nd_before] = (s2[j, r].astype(F32) + z1recv[j].astype(F32)).astype(BF)
            z2copy(j - nd_before).start()

    hidden_ready(0)
    weight_ready(2, down_hbm, dw)

    extra = each(gate_up_own, nj, 1) + each(hidden, nj, 1)

    @pl.loop(0, nd_before)
    def _(step):
        down(0, step)
        reduce_steps(step)
        for i, item in enumerate(extra):
            pl.when(step == min(i + 1, nd_before - 1))(item)

    hidden_ready(1)

    @pl.loop(nd_before, nd_before + nd)
    def _(step):
        down(1, step)
        reduce_steps(step)

    if nd_before < nd:

        @pl.loop(nd_before + nd, total_steps)
        def _(step):
            down(0, step, False)
            reduce_steps(step)

    @pl.loop(total_steps, total_steps + Z_LAG)
    def _(step):
        reduce_steps(step)

    for j in range(nd):
        near_at = j if j < nd_before else j + nd
        z1copy(near_at).wait_recv()
        z2copy(j).wait_recv()
        total = s2[near_at, r].astype(F32) + z1recv[near_at].astype(F32) + z2recv[j].astype(F32)
        out_ref[:, pl.ds(j * dc, dc)] = total.astype(BF)

    def sent(ref, sem):
        pltpu.make_async_copy(ref, ref, sem).wait()

    sent(G.at[pl.ds(0, (3 + A * (2 * B - 1)) * tok)], gs)
    sent(ysend, ys)
    sent(hid.at[:, :, pl.ds(0, F - FT)], hs)
    sent(crecv, cs)
    sent(xrecv, xs)
    sent(z1recv, z1s)
    sent(z2recv, z2s)


def shards(tokens, routes, route_logits, gate_weight, up_weight, down_weight):
    E = lax.axis_size("expert")
    T = lax.axis_size("tensor")
    tok, D = tokens.shape
    top = routes.shape[1]
    _, Dl, F = gate_weight.shape
    cap = tok // 2
    A = 4
    B = E // (2 * A)
    assert E == A * B * 2 and D == Dl * T
    lanes = -(-2 * E // 128) * 128
    hc = 4 if Dl % (4 * 128) == 0 else 1
    nd = 7 if Dl % (7 * 128) == 0 else 1
    dc = Dl // nd
    FT = F // T
    fc = 256 if FT % 256 == 0 else FT
    nj = FT // fc
    pieces = 4
    NG, RG = 4 * B * tok, 4 * B * cap
    dims = (E, T, A, B, tok, cap, top, Dl, F, lanes, hc, nd, dc, fc, nj, pieces)
    vmem = pl.BlockSpec(memory_space=pltpu.VMEM)
    hbm = pl.BlockSpec(memory_space=pl.ANY)
    dma = pltpu.SemaphoreType.DMA
    return pl.pallas_call(
        functools.partial(kernel, dims),
        out_shape=pltpu.VMEM((tok, Dl), BF),
        in_specs=[hbm] * 6,
        out_specs=vmem,
        scratch_shapes=[
            pltpu.VMEM((top, tok), jnp.int32),
            pltpu.VMEM((top, tok), F32),
            pltpu.VMEM((2 * NG, lanes + Dl), BF),
            pltpu.VMEM((Dl, F), BF),
            pltpu.VMEM((Dl, F), BF),
            pltpu.VMEM((Dl, F), BF),
            pltpu.VMEM((2, RG, Dl), BF),
            pltpu.VMEM((2, NG, RG), BF),
            pltpu.VMEM((2, 1, RG), F32),
            pltpu.VMEM((2, T - 1, nj, 2, RG, fc), BF),
            pltpu.VMEM((2, T - 1, nj, 2, RG, fc), BF),
            pltpu.VMEM((2, nj, 2, RG, fc), F32),
            pltpu.VMEM((2, RG, F), BF),
            pltpu.VMEM((2 * nd, 2, NG // 2, dc), BF),
            pltpu.VMEM((2 * nd, NG // 2, dc), BF),
            pltpu.VMEM((2 * nd, B, 2 * tok, dc), BF),
            pltpu.VMEM((2 * nd, B - 1, 2 * tok, dc), BF),
            pltpu.VMEM((2 * nd, 2, tok, dc), BF),
            pltpu.VMEM((2 * nd, tok, dc), BF),
            pltpu.VMEM((nd, tok, dc), BF),
            pltpu.VMEM((nd, tok, dc), BF),
            dma((2,)),
            dma((3,)),
            dma((hc,)),
            dma,
            dma((3, hc)),
            dma((A, B - 1, hc)),
            dma((2, hc)),
            dma,
            dma((2, T - 1, nj)),
            dma,
            dma((2,)),
            dma,
            dma((2 * nd,)),
            dma,
            dma((2 * nd,)),
            dma,
            dma((2 * nd,)),
            dma,
            dma((nd,)),
        ],
        compiler_params=pltpu.CompilerParams(
            collective_id=0, has_side_effects=True, vmem_limit_bytes=60 * 1024 * 1024
        ),
    )(tokens, routes.T, route_logits.T, gate_weight, up_weight, down_weight)


def solution(mesh):
    return jax.shard_map(
        shards,
        mesh=mesh,
        in_specs=(
            P("expert", None),
            P("expert", None),
            P("expert", None),
            P("expert", "tensor", None),
            P("expert", "tensor", None),
            P("expert", "tensor", None),
        ),
        out_specs=P("expert", "tensor"),
        check_vma=False,
    )
```

time: 54.8 us -> 49.4 us (0.901)
  Pallas kernels: 53.1 us -> 48.6 us
  local copies, waits for them, and re-layouts: 1.55 us -> 0.65 us
    pallas_call x1, Pallas kernels: 53.1 us -> 48.6 us  [shards(): pl.pallas_call(functools.partial(kernel, dims), out_shape=pltpu.VMEM((tok...]
    unnamed x1, local copies, waits for them, and re-layouts: 1.55 us -> 0.65 us
where the time goes in v2:
time: 49.4 us; the launch traced here: 49.2 us
  Pallas kernels  48.6 us (98%)
  local copies, waits for them, and re-layouts  0.65 us (1%)
    pallas_call x1, Pallas kernels, shards(): pl.pallas_call(functools.partial(kernel, dims), out_shape=pltpu.VMEM((tok...  48.6 us

profile of v2, /device:TPU:0, one launch (start us, length us, event | category | flops | bytes accessed | tf_op | source)
XLA Modules:
  0.0 49.2 jit_solution(10751089777535627297)
XLA Ops:
  0.0 48.6 %shard_map.64 = bf16[16,3584]{1,0:T(8,128)(2,1)S(1)} custom-call(bf16[16,7168]{1,0:T(8,128)(2,1)} %tokens_ref.1, s32[8,16]{1,0:T(8,128)} %bitcast.2, f32[8,16]{1,0:T(8,128)} %bitcast.3, bf16[1,3584,1024]{2,1,0:T(8,128)(2,1)} %gate_hbm.1, bf16[1,3584,1024]{2,1,0:T(8,128)(2,1)} %up_hbm.1, bf16[1,3584,1024]{2,1,0:T(8,128)(2,1)} %down_hbm.1), custom_call_target="tpu_custom_call" | custom-call | tf_op jit(solution)/shard_map/pallas_call | solution.py:475
  48.6 0.6 %copy.8 = bf16[16,3584]{1,0:T(8,128)(2,1)} copy(bf16[16,3584]{1,0:T(8,128)(2,1)S(1)} %shard_map.64) | data formatting | bytes 229376

commit v3 on v2

--- a/solution.py
+++ b/solution.py
@@ -33,11 +33,13 @@
     dw,
     X,
     spread_back,
-    wslot,
+    wcol,
     ysend,
     yrecv,
     acc,
+    kept_part,
     hid,
+    hid_rows,
     dense,
     crecv,
     s1,
@@ -52,6 +54,7 @@
     gs,
     gzr,
     gxr,
+    gvr,
     gcr,
     ys,
     yr,
@@ -162,21 +165,37 @@
         span = G.at[pl.ds(0, count * tok), part(h)]
         pltpu.make_async_copy(span, span, sem).wait()
 
+    def by_z(h):
+        return h % 2 == 1
+
     def across(i, h):
         slot = slot_of(places[i], b, c)
-        for k in range(1, B):
+        for k in range(1, B) if i < 3 or not by_z(h) else ():
             gcopy(slot, h, dev(a, around(b, k, B), c), gxr.at[i, k - 1, h]).start()
         gcopy(slot, h, sibling, gcr.at[i // 2, h]).start()
 
     def relay(i, h):
         for k in range(1, B):
-            gwait(h, gxr.at[i, k - 1, h])
-            gcopy(slot_of(places[i], around(b, B - k, B), c), h, sibling, gcr.at[i // 2, h]).start()
+            sem = gvr.at[k - 1, h] if i == 3 and by_z(h) else gxr.at[i, k - 1, h]
+            slot = slot_of(places[i], around(b, B - k, B), c)
+            gwait(h, sem)
+            if i == 2 and by_z(h):
+                gcopy(slot, h, z1, gvr.at[k - 1, h]).start()
+            gcopy(slot, h, sibling, gcr.at[i // 2, h]).start()
 
     for h in range(hc):
         token_copies[h].wait()
         gcopy(e, h, z1, gzr.at[0, h]).start()
         across(0, h)
+
+    def own_far(h):
+        gcopy(e, h, z2, gzr.at[1, h]).start()
+
+    @pl.when(r == half)
+    def _():
+        for h in range(hc):
+            own_far(h)
+
 
     step_in = Dl // pieces
     for which, (src, dst) in enumerate(((gate_hbm, gw), (up_hbm, uw), (down_hbm, dw))):
@@ -190,7 +209,7 @@
     for h in range(hc):
         gwait(h, gzr.at[0, h])
         across(1, h)
-        gcopy(e, h, z2, gzr.at[1, h]).start()
+        pl.when(r != half)(functools.partial(own_far, h))
         relay(0, h)
 
     for h in range(hc):
@@ -232,8 +251,7 @@
         slot_col = lax.broadcasted_iota(jnp.int32, (NG, RG), 1).astype(F32)
         spread_back[g] = jnp.where(slot_col == col_at, 1.0, 0.0).astype(BF)
         mine = (at == e) | (at == e + low_at)
-        wcol = jnp.sum(jnp.where(mine, full, 0.0), axis=1, keepdims=True)
-        wslot[g] = jnp.sum(jnp.where(slot_col == col_at, wcol, 0.0), axis=0, keepdims=True)
+        wcol[g] = jnp.sum(jnp.where(mine, full, 0.0), axis=1, keepdims=True)
         return S
 
     chosen = [None, None]
@@ -268,12 +286,23 @@
             device_id_type=MESH,
         )
 
-    def gate_up_theirs(g, j):
+    def gate_up_theirs(g, j, first=0, kept=False):
+        depth = pl.ds(first, Dl - first)
         for p in range(1, T):
             cols = hcols(around(t, p, T), j)
-            ysend[g, p - 1, j, 0] = jnp.dot(X[g], gw[:, cols], preferred_element_type=F32).astype(BF)
-            ysend[g, p - 1, j, 1] = jnp.dot(X[g], uw[:, cols], preferred_element_type=F32).astype(BF)
+            for which, w in enumerate((gw, uw)):
+                value = jnp.dot(X[g, :, depth], w[depth, cols], preferred_element_type=F32)
+                if kept:
+                    value += kept_part[p - 1, j, which]
+                ysend[g, p - 1, j, which] = value.astype(BF)
             ycopy(g, p, j).start()
+
+    def gate_up_part(g, j, until):
+        depth = pl.ds(0, until)
+        for p in range(1, T):
+            cols = hcols(around(t, p, T), j)
+            for which, w in enumerate((gw, uw)):
+                kept_part[p - 1, j, which] = jnp.dot(X[g, :, depth], w[depth, cols], preferred_element_type=F32)
 
     def gate_up_own(g, j):
         cols = hcols(t, j)
@@ -293,28 +322,37 @@
     def hidden_ready(g):
         span = hid.at[g, :, pl.ds(0, F - FT)]
         pltpu.make_async_copy(span, span, hr.at[g]).wait()
-
-    def spread_over(work, side):
-        for i, item in enumerate(work):
-            item()
-            for other in side[i * len(side) // len(work) : (i + 1) * len(side) // len(work)]:
-                other()
-
-    def each(fn, n, *lead):
-        return [functools.partial(fn, *lead, i) for i in range(n)]
+        hid_rows[g] = jnp.dot(spread_back[g], hid[g], preferred_element_type=F32).astype(BF)
 
     for h in range(hc):
         collect(0, h)
     weight_ready(0, gate_hbm, gw)
     weight_ready(1, up_hbm, uw)
-    spread_over(each(gate_up_theirs, nj, 0), each(relay_far, hc))
-    for j in range(nj):
-        gate_up_own(0, j)
-    spread_over(each(relay_last, hc), each(hidden, nj, 0))
-    for h in range(hc):
+    def run(*items):
+        for item in items:
+            item()
+
+    def each(fn, n, *lead):
+        return [functools.partial(fn, *lead, i) for i in range(n)]
+
+    last, finish = each(relay_last, hc), each(hidden, nj, 0)
+    cut = hc // 2
+    run(*each(gate_up_theirs, nj, 0))
+    run(*each(relay_far, hc))
+    run(*each(gate_up_own, nj, 0))
+    run(*last[:cut])
+    run(*finish[:1])
+    run(*last[cut:])
+    for h in range(cut):
+        collect(1, h)
+    run(*finish[1:])
+    for j in range(nj if cut else 0):
+        gate_up_part(1, j, cut * hw)
+    for h in range(cut, hc):
         collect(1, h)
     for j in range(nj):
-        gate_up_theirs(1, j)
+        gate_up_theirs(1, j, cut * hw, bool(cut))
+    run(*each(gate_up_own, nj, 1))
 
     def ccopy(j):
         return pltpu.make_async_remote_copy(
@@ -359,12 +397,11 @@
     total_steps = 2 * nd
     nd_before = max(nd - HELD, 1)
 
-    def down(g, step, early=True):
-        j = step - nd_before if g else step if early else step - nd
+    def down(g, step, first=True):
+        j = step - nd_before if g else step if first else step - nd
         rows = pl.ds(pl.multiple_of(j * dc, 128), dc)
-        y = lax.dot_general(dw[rows, :], hid[g], NT_DIMS, preferred_element_type=F32)
-        y = (y * wslot[g]).astype(BF)
-        y = lax.dot_general(spread_back[g], y, NT_DIMS, preferred_element_type=F32).astype(BF)
+        y = lax.dot_general(hid_rows[g], dw[rows, :], NT_DIMS, preferred_element_type=F32)
+        y = (y * wcol[g]).astype(BF)
         for slot in range(slots):
             at = (slot // 2 % B) * 2 + slot // (2 * B)
             dense[step, slot % 2, at * tok : (at + 1) * tok, :] = y[slot * tok : (slot + 1) * tok]
@@ -403,14 +440,14 @@
     hidden_ready(0)
     weight_ready(2, down_hbm, dw)
 
-    extra = each(gate_up_own, nj, 1) + each(hidden, nj, 1)
+    finish = each(hidden, nj, 1)
 
     @pl.loop(0, nd_before)
     def _(step):
         down(0, step)
         reduce_steps(step)
-        for i, item in enumerate(extra):
-            pl.when(step == min(i + 1, nd_before - 1))(item)
+        for i, item in enumerate(finish):
+            pl.when(step == min(1 + i, nd_before - 1))(item)
 
     hidden_ready(1)
 
@@ -486,11 +523,13 @@
             pltpu.VMEM((Dl, F), BF),
             pltpu.VMEM((2, RG, Dl), BF),
             pltpu.VMEM((2, NG, RG), BF),
-            pltpu.VMEM((2, 1, RG), F32),
+            pltpu.VMEM((2, NG, 1), F32),
             pltpu.VMEM((2, T - 1, nj, 2, RG, fc), BF),
             pltpu.VMEM((2, T - 1, nj, 2, RG, fc), BF),
             pltpu.VMEM((2, nj, 2, RG, fc), F32),
+            pltpu.VMEM((T - 1, nj, 2, RG, fc), F32),
             pltpu.VMEM((2, RG, F), BF),
+            pltpu.VMEM((2, NG, F), BF),
             pltpu.VMEM((2 * nd, 2, NG // 2, dc), BF),
             pltpu.VMEM((2 * nd, NG // 2, dc), BF),
             pltpu.VMEM((2 * nd, B, 2 * tok, dc), BF),
@@ -505,6 +544,7 @@
             dma,
             dma((3, hc)),
             dma((A, B - 1, hc)),
+            dma((B - 1, hc)),
             dma((2, hc)),
             dma,
             dma((2, T - 1, nj)),

time: 49.4 us -> 47.7 us (0.966)
  Pallas kernels: 48.6 us -> 46.9 us
    pallas_call x1, Pallas kernels: 48.6 us -> 46.9 us  [shards(): pl.pallas_call(functools.partial(kernel, dims), out_shape=pltpu.VMEM((tok...]
where the time goes in v3:
time: 47.7 us; the launch traced here: 47.6 us
  Pallas kernels  46.9 us (98%)
  local copies, waits for them, and re-layouts  0.65 us (1%)
    pallas_call x1, Pallas kernels, shards(): pl.pallas_call(functools.partial(kernel, dims), out_shape=pltpu.VMEM((tok...  46.9 us

profile of v3, /device:TPU:0, one launch (start us, length us, event | category | flops | bytes accessed | tf_op | source)
XLA Modules:
  0.0 47.6 jit_solution(3081410949150766694)
XLA Ops:
  0.0 46.9 %shard_map.64 = bf16[16,3584]{1,0:T(8,128)(2,1)S(1)} custom-call(bf16[16,7168]{1,0:T(8,128)(2,1)} %tokens_ref.1, s32[8,16]{1,0:T(8,128)} %bitcast.2, f32[8,16]{1,0:T(8,128)} %bitcast.3, bf16[1,3584,1024]{2,1,0:T(8,128)(2,1)} %gate_hbm.1, bf16[1,3584,1024]{2,1,0:T(8,128)(2,1)} %up_hbm.1, bf16[1,3584,1024]{2,1,0:T(8,128)(2,1)} %down_hbm.1), custom_call_target="tpu_custom_call" | custom-call | tf_op jit(solution)/shard_map/pallas_call | solution.py:512
  46.9 0.6 %copy.8 = bf16[16,3584]{1,0:T(8,128)(2,1)} copy(bf16[16,3584]{1,0:T(8,128)(2,1)S(1)} %shard_map.64) | data formatting | bytes 229376

commit v4 on v3

--- a/solution.py
+++ b/solution.py
@@ -12,8 +12,7 @@
 BF = jnp.bfloat16
 F32 = jnp.float32
 NT_DIMS = (((1,), (1,)), ((), ()))
-CORE_LAG, X_LAG, Z_LAG = 2, 6, 9
-HELD = 0
+CORE_LAG, X_LAG, Z_LAG = 2, 7, 10
 
 
 def kernel(
@@ -395,72 +394,90 @@
         )
 
     total_steps = 2 * nd
-    nd_before = max(nd - HELD, 1)
-
-    def down(g, step, first=True):
-        j = step - nd_before if g else step if first else step - nd
+
+    def down(g, step):
+        j = step - g * nd
         rows = pl.ds(pl.multiple_of(j * dc, 128), dc)
         y = lax.dot_general(hid_rows[g], dw[rows, :], NT_DIMS, preferred_element_type=F32)
         y = (y * wcol[g]).astype(BF)
         for slot in range(slots):
             at = (slot // 2 % B) * 2 + slot // (2 * B)
             dense[step, slot % 2, at * tok : (at + 1) * tok, :] = y[slot * tok : (slot + 1) * tok]
-        ccopy(step).start()
+
+    def core_add(j):
+        for k in range(B):
+            at = pl.ds(k * 2 * tok, 2 * tok)
+            s1[j, k] = (dense[j, c, at].astype(F32) + crecv[j, at].astype(F32)).astype(BF)
+
+    def x_send(j):
+        for k in range(1, B):
+            xcopy(j, k).start()
+
+    def x_wait(j):
+        pltpu.make_async_copy(xrecv.at[j], xrecv.at[j], xr.at[j]).wait()
+
+    def x_add(j):
+        for i in range(2):
+            at = pl.ds(i * tok, tok)
+            total = s1[j, b, at].astype(F32)
+            for k in range(1, B):
+                total += xrecv[j, k - 1, at].astype(F32)
+            s2[j, i] = total.astype(BF)
 
     def reduce_steps(step):
         @pl.when((step >= CORE_LAG) & (step < total_steps + CORE_LAG))
         def _():
             j = step - CORE_LAG
             ccopy(j).wait_recv()
-            for k in range(B):
-                at = pl.ds(k * 2 * tok, 2 * tok)
-                s1[j, k] = (dense[j, c, at].astype(F32) + crecv[j, at].astype(F32)).astype(BF)
-            for k in range(1, B):
-                xcopy(j, k).start()
+            core_add(j)
+            x_send(j)
 
         @pl.when((step >= X_LAG) & (step < total_steps + X_LAG))
         def _():
             j = step - X_LAG
-            pltpu.make_async_copy(xrecv.at[j], xrecv.at[j], xr.at[j]).wait()
-            for i in range(2):
-                at = pl.ds(i * tok, tok)
-                total = s1[j, b, at].astype(F32)
-                for k in range(1, B):
-                    total += xrecv[j, k - 1, at].astype(F32)
-                s2[j, i] = total.astype(BF)
+            x_wait(j)
+            x_add(j)
             z1copy(j).start()
 
-        @pl.when((step >= Z_LAG + nd_before) & (step < nd_before + nd + Z_LAG))
+        @pl.when((step >= Z_LAG + nd) & (step < nd + nd + Z_LAG))
         def _():
             j = step - Z_LAG
             z1copy(j).wait_recv()
-            s3[j - nd_before] = (s2[j, r].astype(F32) + z1recv[j].astype(F32)).astype(BF)
-            z2copy(j - nd_before).start()
+            s3[j - nd] = (s2[j, r].astype(F32) + z1recv[j].astype(F32)).astype(BF)
+            z2copy(j - nd).start()
 
     hidden_ready(0)
     weight_ready(2, down_hbm, dw)
 
     finish = each(hidden, nj, 1)
 
-    @pl.loop(0, nd_before)
+    @pl.loop(0, nd)
     def _(step):
         down(0, step)
+        ccopy(step).start()
         reduce_steps(step)
         for i, item in enumerate(finish):
-            pl.when(step == min(1 + i, nd_before - 1))(item)
+            pl.when(step == min(1 + i, nd - 1))(item)
 
     hidden_ready(1)
 
-    @pl.loop(nd_before, nd_before + nd)
+    steady = X_LAG <= nd <= Z_LAG
+
+    @pl.loop(nd, total_steps)
     def _(step):
-        down(1, step)
-        reduce_steps(step)
-
-    if nd_before < nd:
-
-        @pl.loop(nd_before + nd, total_steps)
-        def _(step):
-            down(0, step, False)
+        if steady:
+            jc, jx = step - CORE_LAG, step - X_LAG
+            ccopy(jc).wait_recv()
+            x_wait(jx)
+            core_add(jc)
+            x_add(jx)
+            down(1, step)
+            ccopy(step).start()
+            x_send(jc)
+            z1copy(jx).start()
+        else:
+            down(1, step)
+            ccopy(step).start()
             reduce_steps(step)
 
     @pl.loop(total_steps, total_steps + Z_LAG)
@@ -468,10 +485,9 @@
         reduce_steps(step)
 
     for j in range(nd):
-        near_at = j if j < nd_before else j + nd
-        z1copy(near_at).wait_recv()
+        z1copy(j).wait_recv()
         z2copy(j).wait_recv()
-        total = s2[near_at, r].astype(F32) + z1recv[near_at].astype(F32) + z2recv[j].astype(F32)
+        total = s2[j, r].astype(F32) + z1recv[j].astype(F32) + z2recv[j].astype(F32)
         out_ref[:, pl.ds(j * dc, dc)] = total.astype(BF)
 
     def sent(ref, sem):

time: 47.7 us -> 48 us (level)
  no operation moved by 1% of the time
where the time goes in v4:
time: 48 us; the launch traced here: 47.8 us
  Pallas kernels  47.1 us (98%)
  local copies, waits for them, and re-layouts  0.65 us (1%)
    pallas_call x1, Pallas kernels, shards(): pl.pallas_call(functools.partial(kernel, dims), out_shape=pltpu.VMEM((tok...  47.1 us

profile of v4, /device:TPU:0, one launch (start us, length us, event | category | flops | bytes accessed | tf_op | source)
XLA Modules:
  0.0 47.8 jit_solution(8010386711552026270)
XLA Ops:
  0.0 47.1 %shard_map.64 = bf16[16,3584]{1,0:T(8,128)(2,1)S(1)} custom-call(bf16[16,7168]{1,0:T(8,128)(2,1)} %tokens_ref.1, s32[8,16]{1,0:T(8,128)} %bitcast.2, f32[8,16]{1,0:T(8,128)} %bitcast.3, bf16[1,3584,1024]{2,1,0:T(8,128)(2,1)} %gate_hbm.1, bf16[1,3584,1024]{2,1,0:T(8,128)(2,1)} %up_hbm.1, bf16[1,3584,1024]{2,1,0:T(8,128)(2,1)} %down_hbm.1), custom_call_target="tpu_custom_call" | custom-call | tf_op jit(solution)/shard_map/pallas_call | solution.py:528
  47.1 0.6 %copy.8 = bf16[16,3584]{1,0:T(8,128)(2,1)} copy(bf16[16,3584]{1,0:T(8,128)(2,1)S(1)} %shard_map.64) | data formatting | bytes 229376
